TPU v7x, 32 devices: a whole 2x2x4 slice. The times are simulated.
32 devices in a mesh: expert: 4 (over x, core), shard: 8 (over z, y).
Axes of the slice: x: 2, y: 2, z: 4, core: 2. Of those that a mesh axis runs over, the one named last changes fastest.
Arguments:
- train_down: float32 [16, 6400, 4096], P('expert', None, 'shard'), may hold values from -0.109375 to 0.109375
- other_down: bfloat16 [16, 6400, 4096], P('expert', None, 'shard'), may hold values from -0.0390625 to 0.0390625
- router_weight: float32 [4096, 16], P('shard', 'expert'), may hold values from -0.09375 to 0.09375
- router_gain: float32 [4096], P('shard'), may hold values from 0.25 to 1.75
Outputs:
- ready_down: bfloat16 [16, 6400, 4096], P('expert', 'shard')
- scale_down: float32 [16, 6400], P('expert', 'shard')
- serve_router: bfloat16 [4096, 16], replicated
All inputs are finite; a program needn't handle non-finite values. Where the computation divides by a largest or mean magnitude, that divisor is 1e-20 or more.
Results may differ from a plain program's by a relative error of at most 0.001.
Values may be sent and summed in bfloat16 or wider, within the bound.
A program may use at most 256 MiB of HBM per device.

v0:
```python
import jax
import jax.numpy as jnp
from jax import lax
from jax.sharding import PartitionSpec as P


def per_device(train_down, other_down, router_weight, router_gain):
    latest_down = train_down + other_down.astype(jnp.float32)
    scale_down = lax.pmax(jnp.max(jnp.abs(latest_down), axis=2), "shard")
    narrow_down = (latest_down / jnp.expand_dims(scale_down, 2)).astype(jnp.bfloat16)
    ready_down = lax.all_to_all(narrow_down, "shard", split_axis=1, concat_axis=2, tiled=True)
    scale_down = lax.dynamic_slice_in_dim(
        scale_down, lax.axis_index("shard") * ready_down.shape[1], ready_down.shape[1], axis=1
    )
    part_router = (router_weight * router_gain[:, None]).astype(jnp.bfloat16)
    row_router = lax.all_gather(part_router, "shard", axis=0, tiled=True)
    serve_router = lax.all_gather(row_router, "expert", axis=1, tiled=True)
    return (ready_down, scale_down, serve_router)


def solution(mesh):
    in_specs = (
        P("expert", None, "shard"),
        P("expert", None, "shard"),
        P("shard", "expert"),
        P("shard"),
    )
    out_specs = (P("expert", "shard", None), P("expert", "shard"), P())
    return jax.shard_map(
        per_device, mesh=mesh, in_specs=in_specs, out_specs=out_specs, check_vma=False
    )
```

profile of v0, /device:TPU:0, one launch (start us, length us, event | category | flops | bytes accessed | tf_op | source)
XLA Modules:
  0.0 903.4 jit_solution(8712372053355540380)
XLA Ops:
  7.2 0.0 all-reduce.2.cloned.1.call-start
  7.2 24.2 %abs_reduce_fusion = f32[4,6400]{1,0:T(4,128)S(1)} fusion(f32[4,6400,512]{2,1,0:T(8,128)} %param.4, bf16[4,6400,512]{2,1,0:T(8,128)(2,1)} %param.5), kind=kLoop, calls=%fused_computation.1 | loop fusion | flops 52403200 | bytes 78745600 | tf_op jit(solution)/shard_map/reduce_max | solution.py:9
  31.4 2.3 copy.21
  33.7 0.0 all-reduce.2.cloned.1.call-update
  33.7 135.6 %all-reduce.2.cloned.1.call-done = f32[4,6400]{0,1:T(8,128)} async-done(((f32[4,6400]{0,1:T(8,128)}), f32[4,6400]{0,1:T(8,128)}) %all-reduce.2.cloned.1.call-update) | async-done | bytes 102416 | tf_op jit(solution)/shard_map/pmax | solution.py:9
  169.4 2.4 copy.17
  171.8 34.3 %divide_convert_fusion = bf16[4,6400,512]{2,1,0:T(8,128)(2,1)} fusion(f32[4,6400,512]{2,1,0:T(8,128)} %param.4, bf16[4,6400,512]{2,1,0:T(8,128)(2,1)} %param.5, f32[4,6400]{1,0:T(4,128)S(1)} %copy.17), kind=kLoop, calls=%fused_computation | loop fusion | flops 52428800 | bytes 104960000 | tf_op jit(solution)/shard_map/convert_element_type | solution.py:10
  206.1 33.4 %copy.18 = bf16[4,6400,512]{2,0,1:T(4,128)(2,1)} copy(bf16[4,6400,512]{2,1,0:T(8,128)(2,1)} %divide_convert_fusion) | data formatting | bytes 52428800 | tf_op jit(solution)/shard_map/convert_element_type | solution.py:10
  239.5 0.0 copy-start
  239.5 0.0 copy-start.1
  239.5 6.6 all-to-all-start
  246.1 0.0 copy-done
  246.2 0.0 copy-done.1
  246.2 585.0 %all_gather.6 = bf16[4096,4]{0,1:T(4,128)(2,1)S(1)} all-gather(bf16[512,4]{0,1:T(4,128)(2,1)S(1)} %multiply_convert_fusion), channel_id=1, replica_groups=mesh['expert'=4,'shard'=8] {'shard'}, dimensions={0}, use_global_device_ids=true | all-gather | bytes 36864 | tf_op jit(solution)/shard_map/all_gather | solution.py:16
  831.2 5.4 all-gather
  836.6 0.7 reshape.9
  837.3 1.0 constant_dynamic-slice_fusion
  838.4 0.8 copy.20
  839.1 0.0 all-to-all-done
  839.1 18.2 %copy.19 = bf16[4,800,8,512]{3,2,1,0:T(8,128)(2,1)} copy(bf16[4,800,8,512]{3,0,1,2:T(4,128)(2,1)} %bitcast.1) | data formatting | bytes 52428800 | tf_op jit(solution)/shard_map/all_to_all | solution.py:11
  857.4 39.2 %all_to_all.16 = bf16[4,800,4096]{2,1,0:T(8,128)(2,1)} reshape(bf16[4,800,8,512]{3,2,1,0:T(8,128)(2,1)} %copy.19) | data formatting | bytes 52428800 | tf_op jit(solution)/shard_map/all_to_all | solution.py:11
  (1 shorter events, 0.0 us)
Async XLA Ops:
  7.2 162.2 %all-reduce.2.cloned.1.call-start = ((), (), s32[]{:S(2)}) async-start(), calls=%async_computation.1 | async-start | bytes 6553600 | tf_op jit(solution)/shard_map/pmax | solution.py:9
  239.5 6.7 copy-start
  239.5 6.7 copy-start.1
  239.5 599.6 %all-to-all-start = ((bf16[4,6400,512]{2,0,1:T(4,128)(2,1)}), bf16[4,6400,512]{2,0,1:T(4,128)(2,1)}, u32[]{:S(2)}, u32[]{:S(2)}) async-start(bf16[4,6400,512]{2,0,1:T(4,128)(2,1)} %copy.18), calls=%async_computation | async-start | bytes 52428800 | tf_op jit(solution)/shard_map/all_to_all | solution.py:11
Sparse Core Ops, SparseCore 0:
  33.9 135.4 all-reduce.1
where the time goes:
time: 905 us; the launch traced here: 903 us
  blocking collectives  590 us (65%)
  waiting for transfers between devices  136 us (15%)
  local copies, waits for them, and re-layouts  98 us (11%)
  other arithmetic  58.5 us (6%)
  between operations  14.1 us (2%)
    all_gather x1, blocking collectives, per_device(): row_router = lax.all_gather(part_router, 'shard', axis=0, tiled=True)  585 us
    pmax x1, waiting for transfers between devices, per_device(): scale_down = lax.pmax(jnp.max(jnp.abs(latest_down), axis=2), 'shard')  136 us
    all_to_all x2, local copies, waits for them, and re-layouts, per_device(): lax.all_to_all(narrow_down, 'shard', split_axis=1, concat_axis=2, tiled=T...  57.4 us
    convert_element_type x1, other arithmetic, per_device(): (latest_down / jnp.expand_dims(scale_down, 2)).astype(jnp.bfloat16)  34.3 us
    convert_element_type x1, local copies, waits for them, and re-layouts, per_device(): (latest_down / jnp.expand_dims(scale_down, 2)).astype(jnp.bfloat16)  33.4 us
    reduce_max x1, other arithmetic, per_device(): scale_down = lax.pmax(jnp.max(jnp.abs(latest_down), axis=2), 'shard')  24.2 us
  transfers between devices with their start and end apart: 2, of which 1 were waited for; matrix products, arithmetic and copies ran while one was open for 0% of the time, Pallas kernels for 0%

commit v1 on v0

v1 whole, which is shorter than its diff:
```python
import functools

import jax
import jax.numpy as jnp
from jax import lax
from jax.experimental import pallas as pl
from jax.experimental.pallas import tpu as pltpu
from jax.sharding import PartitionSpec as P

MESH = pl.DeviceIdType.MESH
AHEAD = 2
LANES = 128


def kernel(
    groups, shards, parts,
    train, other, router, gain,
    ready, scale_out, serve,
    tbuf, obuf, stage, lmax, rmax, gown, gmax, rparts, rflip,
    tsem, osem, own_sem, data_send, data_recv, rs_send, rs_recv, ag_send, ag_recv,
    r1_send, r1_recv, r2_send, r2_recv,
):
    me = lax.axis_index("shard")
    group = lax.axis_index("expert")
    experts = train.shape[0]
    slots, _, rows, cols = tbuf.shape
    chunks = experts * parts
    block = rows * parts

    def shard_id(k):
        return lax.rem(me + k, shards)

    def group_id(k):
        return lax.rem(group + k, groups)

    barrier = pltpu.get_barrier_semaphore()
    for k in range(1, shards):
        pl.semaphore_signal(barrier, inc=1, device_id=(group, shard_id(k)), device_id_type=MESH)
    for k in range(1, groups):
        pl.semaphore_signal(barrier, inc=1, device_id=(group_id(k), me), device_id_type=MESH)

    def place(c, d):
        return c // parts, pl.ds(pl.multiple_of(d * block + lax.rem(c, parts) * rows, 8), rows)

    def load(c, d):
        e, span = place(c, d)
        slot = lax.rem(c, slots)
        return (
            pltpu.make_async_copy(train.at[e, span], tbuf.at[slot, d], tsem.at[slot, d]),
            pltpu.make_async_copy(other.at[e, span], obuf.at[slot, d], osem.at[slot, d]),
        )

    def start_load(c):
        def one(d, _):
            for copy in load(c, d):
                copy.start()
            return 0
        lax.fori_loop(0, shards, one, 0)

    def columns_of(d):
        return pl.ds(pl.multiple_of(d * cols, LANES), cols)

    def send(src, dst, send_sem, recv_sem, peer):
        return pltpu.make_async_remote_copy(
            src_ref=src, dst_ref=dst, send_sem=send_sem, recv_sem=recv_sem,
            device_id=(group, peer), device_id_type=MESH,
        )

    def data_copy(c, d):
        e = c // parts
        span = pl.ds(pl.multiple_of(lax.rem(c, parts) * rows, 8), rows)
        return stage.at[c, d], ready.at[e, span, columns_of(me)]

    start_load(0)
    start_load(1)
    pl.semaphore_wait(barrier, shards - 1 + groups - 1)

    rparts[group, me] = router[...] * gain[...]
    for k in range(1, shards):
        send(rparts.at[group, me], rparts.at[group, me], r1_send, r1_recv, shard_id(k)).start()

    def find_max(c):
        slot = lax.rem(c, slots)

        def one(d, _):
            for copy in load(c, d):
                copy.wait()
            best = None
            for j in range(0, cols, LANES):
                at = pl.ds(j, LANES)
                now = jnp.abs(tbuf[slot, d, :, at] + obuf[slot, d, :, at].astype(jnp.float32))
                best = now if best is None else jnp.maximum(best, now)
            lmax[c, d] = jnp.max(best.T, axis=0, keepdims=True)
            return 0
        lax.fori_loop(0, shards, one, 0)

        def tell(k, _):
            peer = shard_id(k)
            send(lmax.at[c, peer], rmax.at[c, me], rs_send.at[c], rs_recv.at[c], peer).start()
            return 0
        lax.fori_loop(1, shards, tell, 0)
        rmax[c, me] = lmax[c, me]

    def merge(c):
        some = rmax.at[c, pl.ds(0, shards - 1)]
        pltpu.make_async_copy(some, some, rs_recv.at[c]).wait()
        best = rmax[c, 0]
        for d in range(1, shards):
            best = jnp.maximum(best, rmax[c, d])
        gown[c] = best
        scale_out[c] = best

        def tell(k, _):
            send(gown.at[c], gmax.at[c, me], ag_send.at[c], ag_recv.at[c], shard_id(k)).start()
            return 0
        lax.fori_loop(1, shards, tell, 0)
        gmax[c, me] = best

    def narrow(c):
        slot = lax.rem(c, slots)
        some = gmax.at[c, pl.ds(0, shards - 1)]
        pltpu.make_async_copy(some, some, ag_recv.at[c]).wait()

        def one(k, _):
            d = lax.rem(me + shards // 2 + k, shards)
            tall = jnp.broadcast_to(gmax[c, d], (LANES, rows)).T
            for j in range(0, cols, LANES):
                at = pl.ds(j, LANES)
                now = tbuf[slot, d, :, at] + obuf[slot, d, :, at].astype(jnp.float32)
                stage[c, d, :, at] = (now / tall).astype(jnp.bfloat16)
            src, dst = data_copy(c, d)

            @pl.when(d != me)
            def _():
                send(src, dst, data_send.at[d], data_recv.at[me], d).start()

            @pl.when(d == me)
            def _():
                pltpu.make_async_copy(src, dst, own_sem).start()
            return 0
        lax.fori_loop(0, shards, one, 0)

    def step(c, _):
        @pl.when(c < chunks)
        def _():
            find_max(c)

        @pl.when((c >= 1) & (c <= chunks))
        def _():
            merge(c - 1)

        @pl.when(c >= AHEAD)
        def _():
            narrow(c - AHEAD)

        @pl.when(c + 2 < chunks)
        def _():
            start_load(c + 2)
        return 0

    lax.fori_loop(0, chunks + AHEAD, step, 0)

    some = rparts.at[0, pl.ds(0, shards - 1)]
    pltpu.make_async_copy(some, some, r1_recv).wait()
    for k in range(1, groups):
        pltpu.make_async_remote_copy(
            src_ref=rparts.at[group], dst_ref=rparts.at[group], send_sem=r2_send, recv_sem=r2_recv,
            device_id=(group_id(k), me), device_id_type=MESH,
        ).start()
    some = rparts.at[pl.ds(0, groups - 1)]
    pltpu.make_async_copy(some, some, r2_recv).wait()
    wide = router.shape[1]
    for d in range(shards):
        for g in range(groups):
            rflip[g * experts:(g + 1) * experts, :] = rparts[g, d]
        serve[d * wide:(d + 1) * wide, :] = rflip[...].T.astype(jnp.bfloat16)

    some = rparts.at[0, pl.ds(0, shards - 1)]
    pltpu.make_async_copy(some, some, r1_send).wait()
    some = rparts.at[pl.ds(0, groups - 1)]
    pltpu.make_async_copy(some, some, r2_send).wait()

    def drain(c, _):
        some = rmax.at[c, pl.ds(0, shards - 1)]
        pltpu.make_async_copy(some, some, rs_send.at[c]).wait()
        pltpu.make_async_copy(some, some, ag_send.at[c]).wait()
        return 0
    lax.fori_loop(0, chunks, drain, 0)

    mine = ready.at[:, :, columns_of(me)]
    pltpu.make_async_copy(mine, mine, own_sem).wait()

    def finish(k, _):
        d = shard_id(k)
        there = ready.at[:, :, columns_of(d)]
        pltpu.make_async_copy(there, there, data_send.at[d]).wait()
        pltpu.make_async_copy(there, there, data_recv.at[d]).wait()
        return 0
    lax.fori_loop(1, shards, finish, 0)


def pieces(block):
    for count in (5, 4, 3, 2):
        if block % (16 * count) == 0:
            return count
    return 1


def per_device(groups, shards, train_down, other_down, router_weight, router_gain):
    experts, height, cols = train_down.shape
    block = height // shards
    parts = pieces(block)
    rows = block // parts
    chunks = experts * parts
    slots = AHEAD + 2
    wide = router_weight.shape[0]
    f32, bf16 = jnp.float32, jnp.bfloat16
    dma = pltpu.SemaphoreType.DMA
    hbm = pl.BlockSpec(memory_space=pl.ANY)
    vmem = pl.BlockSpec(memory_space=pltpu.VMEM)
    ready, scale, serve = pl.pallas_call(
        functools.partial(kernel, groups, shards, parts),
        out_shape=(
            jax.ShapeDtypeStruct((experts, block, cols * shards), bf16),
            jax.ShapeDtypeStruct((chunks, 1, rows), f32),
            jax.ShapeDtypeStruct((wide * shards, experts * groups), bf16),
        ),
        in_specs=[hbm, hbm, vmem, vmem],
        out_specs=(hbm, vmem, vmem),
        scratch_shapes=[
            pltpu.VMEM((slots, shards, rows, cols), f32),
            pltpu.VMEM((slots, shards, rows, cols), bf16),
            pltpu.VMEM((chunks, shards, rows, cols), bf16),
            pltpu.VMEM((chunks, shards, 1, rows), f32),
            pltpu.VMEM((chunks, shards, 1, rows), f32),
            pltpu.VMEM((chunks, 1, rows), f32),
            pltpu.VMEM((chunks, shards, 1, rows), f32),
            pltpu.VMEM((groups, shards, experts, wide), f32),
            pltpu.VMEM((groups * experts, wide), f32),
            dma((slots, shards)), dma((slots, shards)), dma(()),
            dma((shards,)), dma((shards,)),
            dma((chunks,)), dma((chunks,)), dma((chunks,)), dma((chunks,)),
            dma(()), dma(()), dma(()), dma(()),
        ],
        compiler_params=pltpu.CompilerParams(
            collective_id=0, has_side_effects=True, vmem_limit_bytes=62 * 2**20
        ),
    )(train_down, other_down, router_weight.T, router_gain[None, :])
    return ready, scale.reshape(experts, block), serve


def solution(mesh):
    in_specs = (
        P("expert", None, "shard"),
        P("expert", None, "shard"),
        P("shard", "expert"),
        P("shard"),
    )
    out_specs = (P("expert", "shard", None), P("expert", "shard"), P())
    body = functools.partial(per_device, mesh.shape["expert"], mesh.shape["shard"])
    return jax.shard_map(
        body, mesh=mesh, in_specs=in_specs, out_specs=out_specs, check_vma=False
    )
```

time: 905 us -> 609 us (0.67)
  blocking collectives: 590 us -> 0 us
  Pallas kernels: 0 us -> 586 us
  waiting for transfers between devices: 136 us -> 0 us
  local copies, waits for them, and re-layouts: 98 us -> 20.8 us
  other arithmetic: 58.5 us -> 0.78 us
  between operations: 14.1 us -> 0.64 us
    all_gather x2 -> x0, blocking collectives: 590 us -> none  [the longest x1 585 us: per_device(): row_router = lax.all_gather(part_router, 'shard', axis=0, tiled=True)]
    pallas_call x0 -> x1, Pallas kernels: none -> 586 us  [per_device(): pl.pallas_call(functools.partial(kernel, groups, shards, parts), out_shap...]
    pmax x1 -> x0, waiting for transfers between devices: 136 us -> none  [per_device(): scale_down = lax.pmax(jnp.max(jnp.abs(latest_down), axis=2), 'shard')]
    all_to_all x2 -> x0, local copies, waits for them, and re-layouts: 57.4 us -> none  [per_device(): lax.all_to_all(narrow_down, 'shard', split_axis=1, concat_axis=2, tiled=T...]
    convert_element_type x2 -> x0, other arithmetic: 34.3 us -> none  [the longest x1 34.3 us: per_device(): (latest_down / jnp.expand_dims(scale_down, 2)).astype(jnp.bfloat16)]
    convert_element_type x1 -> x0, local copies, waits for them, and re-layouts: 33.4 us -> none  [per_device(): (latest_down / jnp.expand_dims(scale_down, 2)).astype(jnp.bfloat16)]
    reduce_max x1 -> x0, other arithmetic: 24.2 us -> none  [per_device(): scale_down = lax.pmax(jnp.max(jnp.abs(latest_down), axis=2), 'shard')]
    unnamed x7 -> x2, local copies, waits for them, and re-layouts: 3.75 us -> 20.1 us
  transfers between devices with their start and end apart: 2 -> 0, of which waited for: 1 -> 0; matrix products, arithmetic and copies ran while one was open for 0% -> 0% of each run, Pallas kernels for 0% -> 0%
where the time goes in v1:
time: 609 us
  Pallas kernels  586 us (96%)
  local copies, waits for them, and re-layouts  20.8 us (3%)
    pallas_call x1, Pallas kernels, per_device(): pl.pallas_call(functools.partial(kernel, groups, shards, parts), out_shap...  586 us
    unnamed x2, local copies, waits for them, and re-layouts  20.1 us

profile of v1, /device:TPU:0, one launch (start us, length us, event | category | flops | bytes accessed | tf_op | source)
XLA Modules:
  0.0 608.7 jit_solution(12104473608895775337)
XLA Ops:
  0.6 586.4 %shard_map.67 = (bf16[4,800,4096]{2,1,0:T(8,128)(2,1)}, f32[20,1,160]{2,1,0:T(1,128)}, bf16[4096,16]{1,0:T(8,128)(2,1)}) custom-call(f32[4,6400,512]{2,1,0:T(8,128)} %train.1, bf16[4,6400,512]{2,1,0:T(8,128)(2,1)} %other.1, f32[4,512]{1,0:T(4,128)} %bitcast.2, f32[1,512]{1,0:T(1,128)} %bitcast.3), custom_call_target="tpu_custom_call" | custom-call | tf_op jit(solution)/shard_map/pallas_call | solution.py:221
  587.1 0.8 reduce
  587.8 0.7 reshape.9
  588.5 2.2 copy.7
  590.7 17.9 %copy.9 = bf16[4,800,4096]{2,1,0:T(8,128)(2,1)} copy(bf16[4,800,4096]{2,1,0:T(8,128)(2,1)} %get-tuple-element.15) | data formatting | bytes 52428800
